TPU v7x, 128 devices: a whole 4x4x4 slice. The times are simulated.
128 devices in a mesh: ep: 8 (over z, core), fsdp: 16 (over y, x).
Axes of the slice: x: 4, y: 4, z: 4, core: 2. Of those that a mesh axis runs over, the one named last changes fastest.
Arguments:
- train_gate: float32 [64, 2048, 1408], P('ep', 'fsdp'), may hold values from -0.1875 to 0.1875
- train_up: float32 [64, 2048, 1408], P('ep', 'fsdp'), may hold values from -0.1875 to 0.1875
- train_down: float32 [64, 1408, 2048], P('ep', None, 'fsdp'), may hold values from -0.21875 to 0.21875
- router_weight: float32 [2048, 64], P('fsdp', 'ep'), may hold values from -0.125 to 0.125
- router_gain: float32 [2048], P('fsdp'), may hold values from 0.25 to 1.75
Outputs:
- ready_gate: bfloat16 [64, 2048, 1408], P('ep', None, 'fsdp')
- ready_up: bfloat16 [64, 2048, 1408], P('ep', None, 'fsdp')
- ready_down: bfloat16 [64, 1408, 2048], P('ep', 'fsdp')
- scale_gate: float32 [64, 1408], P('ep', 'fsdp')
- scale_up: float32 [64, 1408], P('ep', 'fsdp')
- scale_down: float32 [64, 1408], P('ep', 'fsdp')
- serve_router: bfloat16 [2048, 64], replicated
All inputs are finite; a program needn't handle non-finite values. Where the computation divides by a largest or mean magnitude, that divisor is 1e-20 or more.
Results may differ from a plain program's by a relative error of at most 0.012.
Values may be sent and summed in bfloat16 or wider, within the bound.
A program may use at most 128 MiB of HBM per device.

v0:
```python
import jax
import jax.numpy as jnp
from jax import lax
from jax.sharding import PartitionSpec as P

D_MODEL = 2048


def sent_to_all(shard, axis):
    copies = jnp.broadcast_to(shard, (lax.axis_size(axis), *shard.shape))
    return lax.all_to_all(copies, axis, split_axis=0, concat_axis=0, tiled=True)


def over_copies(shard, axis):
    everything = sent_to_all(shard, axis)
    return jnp.sum(everything.astype(jnp.float32), axis=0)


def in_one_piece(arrays, axis, split_dim, concat_dim, along):
    ends, at = ([], 0)
    for a in arrays[:-1]:
        at += a.shape[along]
        ends.append(at)
    both = jnp.concatenate(arrays, axis=along)
    return tuple(
        jnp.split(
            lax.all_to_all(both, axis, split_axis=split_dim, concat_axis=concat_dim, tiled=True),
            ends,
            axis=along,
        )
    )


def split_up(shard, dim, size):
    before, after = (shard.shape[:dim], shard.shape[dim + 1 :])
    return jnp.moveaxis(shard.reshape(*before, size, -1, *after), dim, 0)


def edges_of(length, count):
    step = length // count
    if step >= 8:
        step -= step % 8
    return [step * k for k in range(1, count)]


def laid_out(parts, dim):
    shape = list(parts.shape[1:])
    shape[dim] *= parts.shape[0]
    return jnp.moveaxis(parts, 0, dim).reshape(shape)


def exchange_in_pieces(shard, axis, pieces, split_dim, concat_dim):
    parts = split_up(shard, split_dim, lax.axis_size(axis))
    split_at = max(range(1, max(2, parts.ndim - 1)), key=lambda d: parts.shape[d])
    finished = []
    for section in jnp.split(parts, edges_of(parts.shape[split_at], pieces), axis=split_at):
        if section.size:
            finished.append(lax.all_to_all(section, axis, split_axis=0, concat_axis=0, tiled=True))
    return laid_out(jnp.concatenate(finished, axis=split_at), concat_dim)


def collect(shard, axis, dim):
    return laid_out(sent_to_all(shard, axis), dim)


def shards(train_gate, train_up, train_down, router_weight, router_gain):
    total_gate, total_up, total_down = (
        over_copies(jnp.sum(jnp.abs(train_gate), axis=1).astype(jnp.bfloat16), "fsdp").astype(
            jnp.float32
        ),
        over_copies(jnp.sum(jnp.abs(train_up), axis=1).astype(jnp.bfloat16), "fsdp").astype(
            jnp.float32
        ),
        over_copies(jnp.sum(jnp.abs(train_down), axis=2).astype(jnp.bfloat16), "fsdp").astype(
            jnp.float32
        ),
    )
    scale_gate = total_gate / D_MODEL
    scale_up = total_up / D_MODEL
    scale_down = total_down / D_MODEL
    narrow_gate, narrow_up, narrow_down = (
        (train_gate / jnp.expand_dims(scale_gate, 1)).astype(jnp.bfloat16),
        (train_up / jnp.expand_dims(scale_up, 1)).astype(jnp.bfloat16),
        (train_down / jnp.expand_dims(scale_down, 2)).astype(jnp.bfloat16),
    )
    ready_gate, ready_up = in_one_piece((narrow_gate, narrow_up), "fsdp", 2, 1, 0)
    ready_down = exchange_in_pieces(narrow_down, "fsdp", 2, 1, 2)
    scale_gate = lax.dynamic_slice_in_dim(
        scale_gate, lax.axis_index("fsdp") * ready_gate.shape[2], ready_gate.shape[2], axis=1
    )
    scale_up = lax.dynamic_slice_in_dim(
        scale_up, lax.axis_index("fsdp") * ready_up.shape[2], ready_up.shape[2], axis=1
    )
    scale_down = lax.dynamic_slice_in_dim(
        scale_down, lax.axis_index("fsdp") * ready_down.shape[1], ready_down.shape[1], axis=1
    )
    part_router = (router_weight * router_gain[:, None]).astype(jnp.bfloat16)
    row_router = collect(part_router, "fsdp", 0)
    serve_router = collect(row_router, "ep", 1)
    return (ready_gate, ready_up, ready_down, scale_gate, scale_up, scale_down, serve_router)


def solution(mesh):
    in_specs = (
        P("ep", "fsdp", None),
        P("ep", "fsdp", None),
        P("ep", None, "fsdp"),
        P("fsdp", "ep"),
        P("fsdp"),
    )
    out_specs = (
        P("ep", None, "fsdp"),
        P("ep", None, "fsdp"),
        P("ep", "fsdp", None),
        P("ep", "fsdp"),
        P("ep", "fsdp"),
        P("ep", "fsdp"),
        P(),
    )
    return jax.shard_map(shards, mesh=mesh, in_specs=in_specs, out_specs=out_specs, check_vma=False)
```

profile of v0, /device:TPU:0, one launch (start us, length us, event | category | flops | bytes accessed | tf_op | source)
XLA Modules:
  0.0 217.0 jit_solution(6295316721826833313)
XLA Ops:
  0.6 0.7 multiply_convert_fusion
  1.3 0.6 broadcast_in_dim.22
  1.9 7.1 %all-to-all-start.6 = ((bf16[16,128,8]{1,2,0:T(8,128)(2,1)}), bf16[16,128,8]{1,2,0:T(8,128)(2,1)S(1)}, u32[]{:S(2)}, u32[]{:S(2)}) async-start(bf16[16,128,8]{1,2,0:T(8,128)(2,1)} %broadcast_in_dim.22), calls=%async_computation.6 | async-start | bytes 65536 | tf_op jit(solution)/shard_map/all_to_all | solution.py:11
  9.1 4.2 %abs_reduce_fusion = bf16[8,1408]{1,0:T(8,128)(2,1)S(1)} fusion(f32[8,1408,128]{2,1,0:T(8,128)} %param.7), kind=kLoop, calls=%fused_computation.2 | loop fusion | flops 2872320 | bytes 5789696 | tf_op jit(solution)/shard_map/reduce_sum | solution.py:74
  13.3 3.4 %all-to-all-done.6 = bf16[16,128,8]{1,2,0:T(8,128)(2,1)S(1)} async-done(((bf16[16,128,8]{1,2,0:T(8,128)(2,1)}), bf16[16,128,8]{1,2,0:T(8,128)(2,1)S(1)}, u32[]{:S(2)}, u32[]{:S(2)}) %all-to-all-start.6) | async-done | bytes 32800 | tf_op jit(solution)/shard_map/all_to_all | solution.py:11
  16.7 0.8 broadcast_in_dim.21
  17.5 3.8 %all-to-all-start.3 = ((bf16[16,8,1408]{2,1,0:T(8,128)(2,1)}), bf16[16,8,1408]{2,1,0:T(8,128)(2,1)S(1)}, u32[]{:S(2)}, u32[]{:S(2)}) async-start(bf16[16,8,1408]{2,1,0:T(8,128)(2,1)} %broadcast_in_dim.21), calls=%async_computation.3 | async-start | bytes 720896 | tf_op jit(solution)/shard_map/all_to_all | solution.py:11
  21.3 3.2 %abs_reduce_fusion.1 = bf16[8,1408]{1,0:T(8,128)(2,1)S(1)} fusion(f32[8,128,1408]{2,1,0:T(8,128)} %param.6), kind=kLoop, calls=%fused_computation.4 | loop fusion | flops 2872320 | bytes 5789696 | tf_op jit(solution)/shard_map/reduce_sum | solution.py:71
  24.5 6.0 %all-to-all-done.3 = bf16[16,8,1408]{2,1,0:T(8,128)(2,1)S(1)} async-done(((bf16[16,8,1408]{2,1,0:T(8,128)(2,1)}), bf16[16,8,1408]{2,1,0:T(8,128)(2,1)S(1)}, u32[]{:S(2)}, u32[]{:S(2)}) %all-to-all-start.3) | async-done | bytes 360480 | tf_op jit(solution)/shard_map/all_to_all | solution.py:11
  30.5 0.7 broadcast_in_dim.23
  31.2 5.3 %all-to-all-start.7 = ((bf16[8,2048,8]{1,2,0:T(8,128)(2,1)}), bf16[8,2048,8]{1,2,0:T(8,128)(2,1)S(1)}, u32[]{:S(2)}, u32[]{:S(2)}) async-start(bf16[8,2048,8]{1,2,0:T(8,128)(2,1)} %broadcast_in_dim.23), calls=%async_computation.7 | async-start | bytes 524288 | tf_op jit(solution)/shard_map/all_to_all | solution.py:11
  36.6 3.2 %abs_reduce_fusion.2 = bf16[8,1408]{1,0:T(8,128)(2,1)S(1)} fusion(f32[8,128,1408]{2,1,0:T(8,128)} %param.5), kind=kLoop, calls=%fused_computation.6 | loop fusion | flops 2872320 | bytes 5789696 | tf_op jit(solution)/shard_map/reduce_sum | solution.py:68
  39.8 0.1 convert_reduce_fusion
  39.8 4.2 %all-to-all-done.7 = bf16[8,2048,8]{1,2,0:T(8,128)(2,1)S(1)} async-done(((bf16[8,2048,8]{1,2,0:T(8,128)(2,1)}), bf16[8,2048,8]{1,2,0:T(8,128)(2,1)S(1)}, u32[]{:S(2)}, u32[]{:S(2)}) %all-to-all-start.7) | async-done | bytes 262176 | tf_op jit(solution)/shard_map/all_to_all | solution.py:11
  44.1 0.8 broadcast_in_dim.20
  44.8 3.5 %all-to-all-start.1 = ((bf16[16,8,1408]{2,1,0:T(8,128)(2,1)}), bf16[16,8,1408]{2,1,0:T(8,128)(2,1)S(1)}, u32[]{:S(2)}, u32[]{:S(2)}) async-start(bf16[16,8,1408]{2,1,0:T(8,128)(2,1)} %broadcast_in_dim.20), calls=%async_computation.1 | async-start | bytes 720896 | tf_op jit(solution)/shard_map/all_to_all | solution.py:11
  48.4 9.6 %all-to-all-done.1 = bf16[16,8,1408]{2,1,0:T(8,128)(2,1)S(1)} async-done(((bf16[16,8,1408]{2,1,0:T(8,128)(2,1)}), bf16[16,8,1408]{2,1,0:T(8,128)(2,1)S(1)}, u32[]{:S(2)}, u32[]{:S(2)}) %all-to-all-start.1) | async-done | bytes 360480 | tf_op jit(solution)/shard_map/all_to_all | solution.py:11
  58.0 0.8 broadcast_in_dim.19
  58.8 4.2 %all-to-all-start = ((bf16[16,8,1408]{2,1,0:T(8,128)(2,1)}), bf16[16,8,1408]{2,1,0:T(8,128)(2,1)}, u32[]{:S(2)}, u32[]{:S(2)}) async-start(bf16[16,8,1408]{2,1,0:T(8,128)(2,1)} %broadcast_in_dim.19), calls=%async_computation | async-start | bytes 720896 | tf_op jit(solution)/shard_map/all_to_all | solution.py:11
  63.0 4.2 %divide_convert_fusion = bf16[8,1408,128]{2,1,0:T(8,128)(2,1)S(1)} fusion(f32[8,1408,128]{2,1,0:T(8,128)} %param.7, f32[8,1408]{1,0:T(8,128)S(1)} %broadcast_multiply_fusion), kind=kLoop, calls=%fused_computation.1 | loop fusion | flops 2883584 | bytes 8695808 | tf_op jit(solution)/shard_map/convert_element_type | solution.py:84
  67.2 0.1 split.24
  67.4 1.2 copy.46
  68.6 3.6 %all-to-all-done = bf16[16,8,1408]{2,1,0:T(8,128)(2,1)} async-done(((bf16[16,8,1408]{2,1,0:T(8,128)(2,1)}), bf16[16,8,1408]{2,1,0:T(8,128)(2,1)}, u32[]{:S(2)}, u32[]{:S(2)}) %all-to-all-start) | async-done | bytes 360480 | tf_op jit(solution)/shard_map/all_to_all | solution.py:11
  72.2 4.4 %all-to-all-start.4 = ((bf16[16,8,40,128]{3,2,1,0:T(8,128)(2,1)}), bf16[16,8,40,128]{3,2,1,0:T(8,128)(2,1)}, u32[]{:S(2)}, u32[]{:S(2)}) async-start(bf16[16,8,40,128]{3,2,1,0:T(8,128)(2,1)} %copy.46), calls=%async_computation.4 | async-start | bytes 2621440 | tf_op jit(solution)/shard_map/all_to_all | solution.py:58
  76.6 6.5 %copy.40 = f32[8,128,1408]{1,0,2:T(8,128)} copy(f32[8,128,1408]{2,1,0:T(8,128)} %param.5) | data formatting | bytes 11534336 | tf_op args[0]
  83.1 6.5 %copy.42 = f32[8,128,1408]{1,0,2:T(8,128)} copy(f32[8,128,1408]{2,1,0:T(8,128)} %param.6) | data formatting | bytes 11534336 | tf_op args[1]
  89.6 1.3 split.25
  90.8 1.0 convert_reduce_fusion.2
  91.9 0.0 copy-start
  91.9 0.3 copy.39
  92.2 0.1 convert_reduce_fusion.1
  92.2 0.3 copy-done
  92.5 0.3 copy.41
  92.8 2.7 %copy.47 = bf16[16,8,48,128]{3,2,1,0:T(8,128)(2,1)} copy(bf16[16,8,48,128]{3,2,0,1:T(8,128)(2,1)} %split.25) | data formatting | bytes 3145728 | tf_op jit(solution)/shard_map/split | solution.py:56
  95.5 0.0 all-to-all-done.4
  95.5 7.1 %all-to-all-start.5 = ((bf16[16,8,48,128]{3,2,1,0:T(8,128)(2,1)}), bf16[16,8,48,128]{3,2,1,0:T(8,128)(2,1)S(1)}, u32[]{:S(2)}, u32[]{:S(2)}) async-start(bf16[16,8,48,128]{3,2,1,0:T(8,128)(2,1)} %copy.47), calls=%async_computation.5 | async-start | bytes 3145728 | tf_op jit(solution)/shard_map/all_to_all | solution.py:58
  102.6 6.4 %divide_convert_fusion.1 = (bf16[8,128,1408]{1,0,2:T(8,128)(2,1)S(1)}, bf16[8,128,1408]{1,0,2:T(8,128)(2,1)S(1)}) fusion(f32[8,128,1408]{1,0,2:T(8,128)} %copy.42, f32[8,1408]{0,1:T(8,128)S(1)} %copy.41, f32[8,128,1408]{1,0,2:T(8,128)} %copy.40, f32[8,1408]{0,1:T(8,128)S(1)} %copy.39), kind=kLoop, calls=%fused_computation.3 | loop fusion | flops 5767168 | bytes 17391616 | tf_op jit(solution)/shard_map/convert_element_type | solution.py:83
  109.0 3.3 %pad_maximum_fusion = bf16[16,128,1408]{1,0,2:T(8,128)(2,1)} fusion(bf16[8,128,1408]{1,0,2:T(8,128)(2,1)S(1)} %get-tuple-element.9, bf16[8,128,1408]{1,0,2:T(8,128)(2,1)S(1)} %get-tuple-element.10), kind=kLoop, calls=%fused_computation | loop fusion | flops 11534336 | bytes 11534336 | tf_op jit(solution)/shard_map/concatenate | solution.py:24
  112.2 11.9 %all-to-all-done.5 = bf16[16,8,48,128]{3,2,1,0:T(8,128)(2,1)S(1)} async-done(((bf16[16,8,48,128]{3,2,1,0:T(8,128)(2,1)}), bf16[16,8,48,128]{3,2,1,0:T(8,128)(2,1)S(1)}, u32[]{:S(2)}, u32[]{:S(2)}) %all-to-all-start.5) | async-done | bytes 1572896 | tf_op jit(solution)/shard_map/all_to_all | solution.py:58
  124.1 4.8 %all-to-all-start.2 = ((bf16[16,128,1408]{1,0,2:T(8,128)(2,1)}), bf16[16,128,1408]{1,0,2:T(8,128)(2,1)}, u32[]{:S(2)}, u32[]{:S(2)}) async-start(bf16[16,128,1408]{1,0,2:T(8,128)(2,1)} %pad_maximum_fusion), calls=%async_computation.2 | async-start | bytes 11534336 | tf_op jit(solution)/shard_map/all_to_all | solution.py:27
  128.9 0.7 constant_dynamic-slice_fusion
  129.5 0.7 constant_dynamic-slice_fusion.1
  130.2 1.4 constant_dynamic-slice_fusion.2
  131.6 3.3 %copy_bitcast_fusion = bf16[8,88,2048]{2,1,0:T(8,128)(2,1)} fusion(bf16[16,8,48,128]{3,2,1,0:T(8,128)(2,1)S(1)} %all-to-all-done.5, bf16[16,8,40,128]{3,2,1,0:T(8,128)(2,1)} %all-to-all-done.4), kind=kLoop, calls=%fused_computation.7 | loop fusion | flops 5767168 | bytes 5767168 | tf_op jit(solution)/shard_map/reshape | solution.py:49
  134.9 71.5 %all-to-all-done.2 = bf16[16,128,1408]{1,0,2:T(8,128)(2,1)} async-done(((bf16[16,128,1408]{1,0,2:T(8,128)(2,1)}), bf16[16,128,1408]{1,0,2:T(8,128)(2,1)}, u32[]{:S(2)}, u32[]{:S(2)}) %all-to-all-start.2) | async-done | bytes 5767200 | tf_op jit(solution)/shard_map/all_to_all | solution.py:27
  206.4 4.1 %copy.43 = bf16[16,128,1408]{1,2,0:T(8,128)(2,1)S(1)} copy(bf16[16,128,1408]{1,0,2:T(8,128)(2,1)} %all-to-all-done.2) | data formatting | bytes 11534336 | tf_op jit(solution)/shard_map/all_to_all | solution.py:27
  210.5 1.0 slice_bitcast_fusion
  211.5 2.4 %copy.55 = bf16[8,16,11,8,128]{4,3,1,2,0:T(8,128)(2,1)} copy(bf16[8,16,11,8,128]{4,3,2,1,0:T(8,128)(2,1)S(1)} %get-tuple-element.7) | data formatting | bytes 5767168 | tf_op jit(solution)/shard_map/split | solution.py:26
  213.9 2.4 %copy.56 = bf16[8,16,11,8,128]{4,3,1,2,0:T(8,128)(2,1)} copy(bf16[8,16,11,8,128]{4,3,2,1,0:T(8,128)(2,1)S(1)} %get-tuple-element.8) | data formatting | bytes 5767168 | tf_op jit(solution)/shard_map/split | solution.py:26
  216.3 0.7 copy.58
  (3 shorter events, 0.0 us)
Async XLA Ops:
  1.9 14.8 %all-to-all-start.6 = ((bf16[16,128,8]{1,2,0:T(8,128)(2,1)}), bf16[16,128,8]{1,2,0:T(8,128)(2,1)S(1)}, u32[]{:S(2)}, u32[]{:S(2)}) async-start(bf16[16,128,8]{1,2,0:T(8,128)(2,1)} %broadcast_in_dim.22), calls=%async_computation.6 | async-start | bytes 65536 | tf_op jit(solution)/shard_map/all_to_all | solution.py:11
  17.5 13.1 %all-to-all-start.3 = ((bf16[16,8,1408]{2,1,0:T(8,128)(2,1)}), bf16[16,8,1408]{2,1,0:T(8,128)(2,1)S(1)}, u32[]{:S(2)}, u32[]{:S(2)}) async-start(bf16[16,8,1408]{2,1,0:T(8,128)(2,1)} %broadcast_in_dim.21), calls=%async_computation.3 | async-start | bytes 720896 | tf_op jit(solution)/shard_map/all_to_all | solution.py:11
  31.2 12.8 %all-to-all-start.7 = ((bf16[8,2048,8]{1,2,0:T(8,128)(2,1)}), bf16[8,2048,8]{1,2,0:T(8,128)(2,1)S(1)}, u32[]{:S(2)}, u32[]{:S(2)}) async-start(bf16[8,2048,8]{1,2,0:T(8,128)(2,1)} %broadcast_in_dim.23), calls=%async_computation.7 | async-start | bytes 524288 | tf_op jit(solution)/shard_map/all_to_all | solution.py:11
  44.8 13.2 %all-to-all-start.1 = ((bf16[16,8,1408]{2,1,0:T(8,128)(2,1)}), bf16[16,8,1408]{2,1,0:T(8,128)(2,1)S(1)}, u32[]{:S(2)}, u32[]{:S(2)}) async-start(bf16[16,8,1408]{2,1,0:T(8,128)(2,1)} %broadcast_in_dim.20), calls=%async_computation.1 | async-start | bytes 720896 | tf_op jit(solution)/shard_map/all_to_all | solution.py:11
  58.8 13.4 %all-to-all-start = ((bf16[16,8,1408]{2,1,0:T(8,128)(2,1)}), bf16[16,8,1408]{2,1,0:T(8,128)(2,1)}, u32[]{:S(2)}, u32[]{:S(2)}) async-start(bf16[16,8,1408]{2,1,0:T(8,128)(2,1)} %broadcast_in_dim.19), calls=%async_computation | async-start | bytes 720896 | tf_op jit(solution)/shard_map/all_to_all | solution.py:11
  72.2 23.3 %all-to-all-start.4 = ((bf16[16,8,40,128]{3,2,1,0:T(8,128)(2,1)}), bf16[16,8,40,128]{3,2,1,0:T(8,128)(2,1)}, u32[]{:S(2)}, u32[]{:S(2)}) async-start(bf16[16,8,40,128]{3,2,1,0:T(8,128)(2,1)} %copy.46), calls=%async_computation.4 | async-start | bytes 2621440 | tf_op jit(solution)/shard_map/all_to_all | solution.py:58
  91.9 0.6 copy-start
  95.5 28.6 %all-to-all-start.5 = ((bf16[16,8,48,128]{3,2,1,0:T(8,128)(2,1)}), bf16[16,8,48,128]{3,2,1,0:T(8,128)(2,1)S(1)}, u32[]{:S(2)}, u32[]{:S(2)}) async-start(bf16[16,8,48,128]{3,2,1,0:T(8,128)(2,1)} %copy.47), calls=%async_computation.5 | async-start | bytes 3145728 | tf_op jit(solution)/shard_map/all_to_all | solution.py:58
  124.1 82.3 %all-to-all-start.2 = ((bf16[16,128,1408]{1,0,2:T(8,128)(2,1)}), bf16[16,128,1408]{1,0,2:T(8,128)(2,1)}, u32[]{:S(2)}, u32[]{:S(2)}) async-start(bf16[16,128,1408]{1,0,2:T(8,128)(2,1)} %pad_maximum_fusion), calls=%async_computation.2 | async-start | bytes 11534336 | tf_op jit(solution)/shard_map/all_to_all | solution.py:27
where the time goes:
time: 219 us; the launch traced here: 217 us
  waiting for transfers between devices  110 us (50%)
  starting transfers between devices  40.3 us (18%)
  local copies, waits for them, and re-layouts  36 us (16%)
  other arithmetic  29.7 us (14%)
    all_to_all x1, waiting for transfers between devices, in_one_piece(): lax.all_to_all(both, axis, split_axis=split_dim, concat_axis=concat_dim,...  71.5 us
    all_to_all x5, waiting for transfers between devices, sent_to_all(): return lax.all_to_all(copies, axis, split_axis=0, concat_axis=0, tiled=True)  26.8 us
    all_to_all x5, starting transfers between devices, sent_to_all(): return lax.all_to_all(copies, axis, split_axis=0, concat_axis=0, tiled=True)  24.1 us
    unnamed x6, local copies, waits for them, and re-layouts  14.9 us
    all_to_all x2, waiting for transfers between devices, exchange_in_pieces(): lax.all_to_all(section, axis, split_axis=0, concat_axis=0, tiled=True)  11.9 us
    all_to_all x2, starting transfers between devices, exchange_in_pieces(): lax.all_to_all(section, axis, split_axis=0, concat_axis=0, tiled=True)  11.5 us
    convert_element_type x1, other arithmetic, shards(): (train_up / jnp.expand_dims(scale_up, 1)).astype(jnp.bfloat16)  6.36 us
    split x4, local copies, waits for them, and re-layouts, exchange_in_pieces(): jnp.split(parts, edges_of(parts.shape[split_at], pieces), axis=split_at)  5.34 us
  transfers between devices with their start and end apart: 8, of which 7 were waited for; matrix products, arithmetic and copies ran while one was open for 23% of the time, Pallas kernels for 0%

commit v1 on v0

v1 whole, which is shorter than its diff:
```python
import functools

import jax
import jax.numpy as jnp
from jax import lax
from jax.experimental import pallas as pl
from jax.experimental.pallas import tpu as pltpu
from jax.sharding import PartitionSpec as P

MESH = pl.DeviceIdType.MESH
MIB = 2**20
AHEAD = 3


def exchange(
    n, groups, rows,
    down, gate, up, router, gain,
    ready, scales, served,
    down_in, wide_in, send, recv, part,
    load_sem, send_sem, recv_sem, row_send, row_recv, col_send, col_recv,
):
    me, mine = lax.axis_index("fsdp"), lax.axis_index("ep")
    experts, tiles = down_in.shape[0], rows // 8
    slab = 128

    barrier = pltpu.get_barrier_semaphore()
    for k in range(1, n):
        pl.semaphore_signal(barrier, inc=1, device_id={"fsdp": lax.rem(me + k, n)}, device_id_type=MESH)
    for k in range(1, groups):
        pl.semaphore_signal(barrier, inc=1, device_id={"ep": lax.rem(mine + k, groups)}, device_id_type=MESH)

    def load(kind, e):
        src = (down, gate, up)[kind].at[e]
        dst = down_in.at[e] if kind == 0 else wide_in.at[(kind - 1) * experts + e]
        return pltpu.make_async_copy(src, dst, load_sem.at[kind * experts + e])

    for e in range(AHEAD):
        load(0, e).start()

    part[...] = (router[...] * gain[...]).astype(jnp.bfloat16)
    served[mine, me] = part[...]

    pl.semaphore_wait(barrier, n + groups - 2)

    def row_copy(k):
        peer = lax.rem(me + k, n)
        return pltpu.make_async_remote_copy(
            src_ref=part, dst_ref=served.at[mine, me], send_sem=row_send, recv_sem=row_recv,
            device_id={"fsdp": peer}, device_id_type=MESH,
        )

    def col_copy(k):
        return pltpu.make_async_remote_copy(
            src_ref=served.at[mine], dst_ref=served.at[mine],
            send_sem=col_send, recv_sem=col_recv,
            device_id={"ep": lax.rem(mine + k, groups)}, device_id_type=MESH,
        )

    def share_copy(p, k):
        peer = lax.rem(me + k, n)
        return pltpu.make_async_remote_copy(
            src_ref=send.at[p, peer], dst_ref=recv.at[p, me],
            send_sem=send_sem.at[p], recv_sem=recv_sem.at[p],
            device_id={"fsdp": peer}, device_id_type=MESH,
        )

    def send_out(p):
        for k in range(1, n):
            share_copy(p, k).start()
        recv[p, me] = send[p, me]

    def narrow_down(e, carry):
        @pl.when(e + AHEAD < experts)
        def _():
            load(0, e + AHEAD).start()

        @pl.when(e + AHEAD >= experts)
        def _():
            load(1, e + AHEAD - experts).start()

        load(0, e).wait()
        for k in range(n):
            x = down_in[e, rows * k : rows * (k + 1), :]
            send[e, k] = x.reshape(tiles, 8, slab).astype(jnp.bfloat16)
        send_out(e)
        return carry

    lax.fori_loop(0, experts, narrow_down, 0)

    for k in range(1, n):
        row_copy(k).start()

    def narrow_wide(kind, e, carry):
        @pl.when(e + AHEAD < experts)
        def _():
            load(kind, e + AHEAD).start()

        if kind == 1:

            @pl.when(e + AHEAD >= experts)
            def _():
                load(2, e + AHEAD - experts).start()

        load(kind, e).wait()
        p = kind * experts + e
        for b in range(rows * n // slab):
            x = wide_in[p - experts, :, slab * b : slab * (b + 1)].T
            for i in range(slab // 8):
                at = (slab * b) // 8 + i
                send[p, at // tiles, at % tiles] = x[8 * i : 8 * (i + 1), :].astype(jnp.bfloat16)
        send_out(p)
        return carry

    lax.fori_loop(0, experts, functools.partial(narrow_wide, 1), 0)

    everyone = served.at[mine, pl.ds(0, n - 1)]
    pltpu.make_async_copy(everyone, everyone, row_recv).wait()
    for k in range(1, groups):
        col_copy(k).start()

    lax.fori_loop(0, experts, functools.partial(narrow_wide, 2), 0)

    def scale(kind, e, carry):
        p = kind * experts + e
        arrived = recv.at[p, pl.ds(0, n - 1)]
        pltpu.make_async_copy(arrived, arrived, recv_sem.at[p]).wait()
        total = jnp.abs(recv[p, 0].astype(jnp.float32))
        for s in range(1, n):
            total += jnp.abs(recv[p, s].astype(jnp.float32))
        mean = jnp.sum(total, axis=2, keepdims=True) * (1.0 / (slab * n))
        inverse = 1.0 / mean
        for s in range(n):
            ready[p, :, s] = (recv[p, s].astype(jnp.float32) * inverse).astype(jnp.bfloat16)
        row = jnp.sum(total.reshape(rows, slab).T, axis=0, keepdims=True)
        scales[kind, pl.ds(e, 1), :] = row * (1.0 / (slab * n))
        return carry

    for kind in range(3):
        lax.fori_loop(0, experts, functools.partial(scale, kind), 0)

    def sent(p, carry):
        gone = send.at[p, pl.ds(0, n - 1)]
        pltpu.make_async_copy(gone, gone, send_sem.at[p]).wait()
        return carry

    lax.fori_loop(0, 3 * experts, sent, 0)
    pltpu.make_async_copy(everyone, everyone, row_send).wait()
    others = served.at[pl.ds(0, groups - 1)]
    pltpu.make_async_copy(others, others, col_send).wait()
    pltpu.make_async_copy(others, others, col_recv).wait()


def write_out(ready, scales, served, out_down, out_gate, out_up, s_down, s_gate, s_up, out_router, sem):
    experts = out_down.shape[0]
    copies = []
    for kind, out in enumerate((out_down, out_gate, out_up)):
        copies.append((ready.at[pl.ds(kind * experts, experts)], out))
    for kind, out in enumerate((s_down, s_gate, s_up)):
        copies.append((scales.at[kind], out))
    copies.append((served, out_router))
    started = [pltpu.make_async_copy(a, b, sem.at[i]) for i, (a, b) in enumerate(copies)]
    for c in started:
        c.start()
    for c in started:
        c.wait()


def shards(train_gate, train_up, train_down, router_weight, router_gain):
    n, groups = lax.axis_size("fsdp"), lax.axis_size("ep")
    experts, d, f = train_gate.shape
    rows = f // n
    tiles = rows // 8
    bf16, f32 = jnp.bfloat16, jnp.float32
    any_, vmem = pl.BlockSpec(memory_space=pl.ANY), pl.BlockSpec(memory_space=pltpu.VMEM)
    ready, scales, served = pl.pallas_call(
        functools.partial(exchange, n, groups, rows),
        out_shape=(
            pltpu.VMEM((3 * experts, tiles, n, 8, d), bf16),
            pltpu.VMEM((3, experts, rows), f32),
            pltpu.VMEM((groups, n, router_weight.shape[1], d), bf16),
        ),
        in_specs=[any_, any_, any_, vmem, vmem],
        out_specs=(vmem, vmem, vmem),
        scratch_shapes=[
            pltpu.VMEM((experts, f, d), f32),
            pltpu.VMEM((2 * experts, d, f), f32),
            pltpu.VMEM((3 * experts, n, tiles, 8, d), bf16),
            pltpu.VMEM((3 * experts, n, tiles, 8, d), bf16),
            pltpu.VMEM((router_weight.shape[1], d), bf16),
            pltpu.SemaphoreType.DMA((3 * experts,)),
            pltpu.SemaphoreType.DMA((3 * experts,)),
            pltpu.SemaphoreType.DMA((3 * experts,)),
            pltpu.SemaphoreType.DMA,
            pltpu.SemaphoreType.DMA,
            pltpu.SemaphoreType.DMA,
            pltpu.SemaphoreType.DMA,
        ],
        compiler_params=pltpu.CompilerParams(
            collective_id=0, has_side_effects=True, vmem_limit_bytes=48 * MIB
        ),
        name="exchange",
    )(train_down, train_gate, train_up, router_weight.T, router_gain.reshape(1, d))
    tile = jax.ShapeDtypeStruct((experts, tiles, n, 8, d), bf16)
    scale = jax.ShapeDtypeStruct((experts, rows), f32)
    down, gate, up, s_down, s_gate, s_up, router = pl.pallas_call(
        write_out,
        out_shape=(tile, tile, tile, scale, scale, scale, jax.ShapeDtypeStruct(served.shape, bf16)),
        in_specs=[vmem, vmem, vmem],
        out_specs=(any_,) * 7,
        scratch_shapes=[pltpu.SemaphoreType.DMA((7,))],
        compiler_params=pltpu.CompilerParams(vmem_limit_bytes=16 * MIB),
        name="write_out",
    )(ready, scales, served)

    def whole(x):
        return x.transpose(0, 1, 3, 2, 4).reshape(experts, rows, n * d)

    serve_router = router.transpose(1, 3, 0, 2).reshape(n * d, -1)
    return (
        whole(gate).swapaxes(1, 2), whole(up).swapaxes(1, 2), whole(down),
        s_gate, s_up, s_down, serve_router,
    )


def solution(mesh):
    in_specs = (
        P("ep", "fsdp", None),
        P("ep", "fsdp", None),
        P("ep", None, "fsdp"),
        P("fsdp", "ep"),
        P("fsdp"),
    )
    out_specs = (
        P("ep", None, "fsdp"),
        P("ep", None, "fsdp"),
        P("ep", "fsdp", None),
        P("ep", "fsdp"),
        P("ep", "fsdp"),
        P("ep", "fsdp"),
        P(),
    )
    return jax.shard_map(shards, mesh=mesh, in_specs=in_specs, out_specs=out_specs, check_vma=False)
```

time: 219 us -> 109 us (0.50)
  waiting for transfers between devices: 110 us -> 0 us
  Pallas kernels: 0 us -> 108 us
  starting transfers between devices: 40.3 us -> 0 us
  local copies, waits for them, and re-layouts: 36 us -> 0 us
  other arithmetic: 29.7 us -> 0 us
    all_to_all x8 -> x0, waiting for transfers between devices: 110 us -> none  [the longest x1 71.5 us: in_one_piece(): lax.all_to_all(both, axis, split_axis=split_dim, concat_axis=concat_dim,...]
    pallas_call x0 -> x2, Pallas kernels: none -> 108 us  [the longest x1 104 us: shards(): pl.pallas_call(functools.partial(exchange, n, groups, rows), out_shape=(p...]
    all_to_all x8 -> x0, starting transfers between devices: 40.3 us -> none  [the longest x5 24.1 us: sent_to_all(): return lax.all_to_all(copies, axis, split_axis=0, concat_axis=0, tiled=True)]
    unnamed x6 -> x0, local copies, waits for them, and re-layouts: 14.9 us -> none
    reduce_sum x6 -> x0, other arithmetic: 11.8 us -> none  [the longest x1 4.2 us: shards(): jnp.sum(jnp.abs(train_down), axis=2).astype(jnp.bfloat16)]
    convert_element_type x3 -> x0, other arithmetic: 11.3 us -> none  [the longest x1 6.36 us: shards(): (train_up / jnp.expand_dims(scale_up, 1)).astype(jnp.bfloat16)]
    split x6 -> x0, local copies, waits for them, and re-layouts: 10.1 us -> none  [the longest x4 5.34 us: exchange_in_pieces(): jnp.split(parts, edges_of(parts.shape[split_at], pieces), axis=split_at)]
    all_to_all x1 -> x0, local copies, waits for them, and re-layouts: 4.12 us -> none  [in_one_piece(): lax.all_to_all(both, axis, split_axis=split_dim, concat_axis=concat_dim,...]
  transfers between devices with their start and end apart: 8 -> 0, of which waited for: 7 -> 0; matrix products, arithmetic and copies ran while one was open for 23% -> 0% of each run, Pallas kernels for 0% -> 0%
where the time goes in v1:
time: 109 us; the launch traced here: 108 us
  Pallas kernels  108 us (99%)
    pallas_call x1, Pallas kernels, shards(): pl.pallas_call(functools.partial(exchange, n, groups, rows), out_shape=(p...  104 us
    pallas_call x1, Pallas kernels, shards(): pl.pallas_call(write_out, out_shape=(tile, tile, tile, scale, scale, scal...  3.55 us

profile of v1, /device:TPU:0, one launch (start us, length us, event | category | flops | bytes accessed | tf_op | source)
XLA Modules:
  0.0 108.5 jit_solution(13223199837417257868)
XLA Ops:
  0.6 104.3 %exchange.1 = (bf16[24,11,16,8,128]{4,3,2,1,0:T(8,128)(2,1)S(1)}, f32[3,8,88]{2,1,0:T(8,128)S(1)}, bf16[8,16,8,128]{3,2,1,0:T(8,128)(2,1)S(1)}) custom-call(f32[8,1408,128]{2,1,0:T(8,128)} %down.1, f32[8,128,1408]{2,1,0:T(8,128)} %gate.1, f32[8,128,1408]{2,1,0:T(8,128)} %up.1, f32[8,128]{1,0:T(8,128)} %bitcast.18, f32[1,128]{1,0:T(1,128)} %bitcast.19), custom_call_target="tpu_custom_call" | custom-call | tf_op jit(solution)/shard_map/exchange/pallas_call | solution.py:175
  104.9 3.5 %write_out.1 = (bf16[8,11,16,8,128]{4,3,2,1,0:T(8,128)(2,1)}, bf16[8,11,16,8,128]{4,3,2,1,0:T(8,128)(2,1)}, bf16[8,11,16,8,128]{4,3,2,1,0:T(8,128)(2,1)}, f32[8,...) custom-call(bf16[24,11,16,8,128]{4,3,2,1,0:T(8,128)(2,1)S(1)} %get-tuple-element.17.ready, ...), custom_call_target="tpu_custom_call" | custom-call | tf_op jit(solution)/shard_map/write_out/pallas_call | solution.py:205

commit v2 on v1

v2 whole, which is shorter than its diff:
```python
import functools

import jax
import jax.numpy as jnp
from jax import lax
from jax.experimental import pallas as pl
from jax.experimental.pallas import tpu as pltpu
from jax.sharding import PartitionSpec as P

MESH = pl.DeviceIdType.MESH
MIB = 2**20
AHEAD = 3


def scaled(arrived, put):
    n, tiles, eight, slab = arrived.shape
    total = jnp.abs(arrived[0].astype(jnp.float32))
    for s in range(1, n):
        total += jnp.abs(arrived[s].astype(jnp.float32))
    mean = jnp.sum(total, axis=2, keepdims=True) * (1.0 / (slab * n))
    inverse = 1.0 / mean
    for s in range(n):
        put(s, (arrived[s].astype(jnp.float32) * inverse).astype(jnp.bfloat16))
    row = jnp.sum(total.reshape(tiles * eight, slab).T, axis=0, keepdims=True)
    return row * (1.0 / (slab * n))


def exchange(
    n, groups, rows,
    down, gate, up, router, gain,
    ready, last, scales, served,
    down_in, wide_in, router_in, gain_in, send, recv, part,
    load_sem, slab_sem, router_sem, send_sem, recv_sem,
    row_send, row_recv, in_send, in_recv, out_send, out_recv,
):
    me, group = lax.axis_index("fsdp"), lax.axis_index("ep")
    experts, tiles, slab = down_in.shape[0], rows // 8, down_in.shape[2]
    bf16 = jnp.bfloat16

    def peer_of(k):
        return lax.rem(me + k, n)

    barrier = pltpu.get_barrier_semaphore()
    for k in range(1, n):
        pl.semaphore_signal(barrier, inc=1, device_id={"fsdp": peer_of(k)}, device_id_type=MESH)

    @pl.when(group == 0)
    def _():
        for g in range(1, groups):
            pl.semaphore_signal(barrier, inc=1, device_id={"ep": g}, device_id_type=MESH)

    def load_slab(k):
        at = pl.ds(pl.multiple_of(peer_of(k) * rows, 8), rows)
        return pltpu.make_async_copy(down.at[0, at], down_in.at[0, at], slab_sem.at[k])

    def load(kind, e):
        src = (down, gate, up)[kind].at[e]
        dst = down_in.at[e] if kind == 0 else wide_in.at[(kind - 1) * experts + e]
        return pltpu.make_async_copy(src, dst, load_sem.at[kind * experts + e])

    for k in range(1, n + 1):
        load_slab(k % n).start()
    for e in range(1, AHEAD):
        load(0, e).start()
    load_router = pltpu.make_async_copy(router, router_in, router_sem.at[0])
    load_gain = pltpu.make_async_copy(gain, gain_in, router_sem.at[1])
    load_router.start()
    load_gain.start()

    def row_copy(k):
        return pltpu.make_async_remote_copy(
            src_ref=part, dst_ref=served.at[group, me], send_sem=row_send, recv_sem=row_recv,
            device_id={"fsdp": peer_of(k)}, device_id_type=MESH,
        )

    def share_copy(p, k):
        peer = peer_of(k)
        return pltpu.make_async_remote_copy(
            src_ref=send.at[p, peer],
            dst_ref=recv.at[p, me],
            send_sem=send_sem.at[p], recv_sem=recv_sem.at[p],
            device_id={"fsdp": peer}, device_id_type=MESH,
        )

    def last_copy(k):
        p, peer = 3 * experts - 1, peer_of(k)
        return pltpu.make_async_remote_copy(
            src_ref=send.at[p, peer], dst_ref=last.at[me],
            send_sem=send_sem.at[p], recv_sem=recv_sem.at[p],
            device_id={"fsdp": peer}, device_id_type=MESH,
        )

    def narrow_slab(e, k):
        x = down_in[e, pl.ds(pl.multiple_of(k * rows, 8), rows), :]
        return x.reshape(tiles, 8, slab).astype(bf16)

    for k in range(1, n):
        load_slab(k).wait()
        send[0, peer_of(k)] = narrow_slab(0, peer_of(k))
        if k == 1:
            pl.semaphore_wait(barrier, n - 1 + jnp.where(group == 0, 0, 1))
        share_copy(0, k).start()
    load_slab(0).wait()
    recv[0, me] = narrow_slab(0, me)

    def narrow_down(e, carry):
        @pl.when(e + AHEAD - 1 < experts)
        def _():
            load(0, e + AHEAD - 1).start()

        @pl.when(e + AHEAD - 1 >= experts)
        def _():
            load(1, e + AHEAD - 1 - experts).start()

        load(0, e).wait()
        for k in range(n):
            send[e, k] = narrow_slab(e, k)
        for k in range(1, n):
            share_copy(e, k).start()
        recv[e, me] = send[e, me]
        return carry

    lax.fori_loop(1, experts, narrow_down, 0)

    load_router.wait()
    load_gain.wait()
    part[...] = (router_in[...] * gain_in[...]).astype(bf16)
    served[group, me] = part[...]
    for k in range(1, n):
        row_copy(k).start()

    def narrow_wide(kind, e):
        load(kind, e).wait()
        p = kind * experts + e
        for b in range(rows * n // slab):
            x = wide_in[p - experts, :, slab * b : slab * (b + 1)].T
            for i in range(slab // 8):
                at = (slab * b) // 8 + i
                send[p, at // tiles, at % tiles] = x[8 * i : 8 * (i + 1), :].astype(bf16)

    def narrow_gate(e, carry):
        @pl.when(e + AHEAD - 1 < experts)
        def _():
            load(1, e + AHEAD - 1).start()

        @pl.when(e + AHEAD - 1 >= experts)
        def _():
            load(2, e + AHEAD - 1 - experts).start()

        narrow_wide(1, e)
        p = experts + e
        for k in range(1, n):
            share_copy(p, k).start()
        recv[p, me] = send[p, me]
        return carry

    lax.fori_loop(0, experts, narrow_gate, 0)

    others = served.at[group, pl.ds(0, n - 1)]
    pltpu.make_async_copy(others, others, row_recv).wait()
    inward = pltpu.make_async_remote_copy(
        src_ref=served.at[group], dst_ref=served.at[group], send_sem=in_send, recv_sem=in_recv,
        device_id={"ep": 0}, device_id_type=MESH,
    )

    def outward(g, j):
        return pltpu.make_async_remote_copy(
            src_ref=served.at[j], dst_ref=served.at[j], send_sem=out_send, recv_sem=out_recv,
            device_id={"ep": g}, device_id_type=MESH,
        )

    @pl.when(group != 0)
    def _():
        inward.start()

    def narrow_up(e, carry):
        @pl.when(e + AHEAD - 1 < experts)
        def _():
            load(2, e + AHEAD - 1).start()

        narrow_wide(2, e)
        p = 2 * experts + e

        @pl.when(e < experts - 1)
        def _():
            for k in range(1, n):
                share_copy(p, k).start()
            recv[p, me] = send[p, me]

        return carry

    lax.fori_loop(0, experts, narrow_up, 0)
    for k in range(1, n):
        last_copy(k).start()
    last[me] = send[3 * experts - 1, me]

    theirs = served.at[pl.ds(0, groups - 1)]

    @pl.when(group == 0)
    def _():
        pltpu.make_async_copy(theirs, theirs, in_recv).wait()
        for g in range(1, groups):
            for j in range(groups):
                if j != g:
                    outward(g, j).start()

    def scale(kind, e, carry):
        p = kind * experts + e
        arrived = recv.at[p, pl.ds(0, n - 1)]
        pltpu.make_async_copy(arrived, arrived, recv_sem.at[p]).wait()

        def put(s, x):
            ready[p, :, s] = x

        scales[kind, pl.ds(e, 1), :] = scaled(recv.at[p], put)
        return carry

    for kind in range(3):
        lax.fori_loop(0, experts - (kind == 2), functools.partial(scale, kind), 0)

    def sent(p, carry):
        gone = send.at[p, pl.ds(0, n - 1)]
        pltpu.make_async_copy(gone, gone, send_sem.at[p]).wait()
        return carry

    lax.fori_loop(0, 3 * experts - 1, sent, 0)
    pltpu.make_async_copy(others, others, row_send).wait()

    @pl.when(group == 0)
    def _():
        for _ in range(1, groups):
            pltpu.make_async_copy(theirs, theirs, out_send).wait()

    @pl.when(group != 0)
    def _():
        mine = served.at[group]
        pltpu.make_async_copy(mine, mine, in_send).wait()
        pltpu.make_async_copy(theirs, theirs, out_recv).wait()

    arrived = last.at[pl.ds(0, n - 1)]
    pltpu.make_async_copy(arrived, arrived, recv_sem.at[3 * experts - 1]).wait()
    sent(3 * experts - 1, 0)


def write_out(ready, last, scales, served, out_down, out_gate, out_up, s_down, s_gate, s_up, out_router, held, row, sem, row_sem):
    experts = out_down.shape[0]
    copies = [(served, out_router), (scales.at[0], s_down), (scales.at[1], s_gate)]
    for kind, out in enumerate((out_down, out_gate, out_up)):
        for e in range(0, experts, 2):
            size = min(2, experts - e - (kind == 2))
            copies.append((ready.at[pl.ds(kind * experts + e, size)], out.at[pl.ds(e, size)]))
    started = [pltpu.make_async_copy(a, b, sem.at[i]) for i, (a, b) in enumerate(copies)]
    for c in started:
        c.start()

    def put(s, x):
        held[:, s] = x

    row[...] = scales[2]
    row[pl.ds(experts - 1, 1), :] = scaled(last, put)
    finish = [
        pltpu.make_async_copy(held, out_up.at[experts - 1], row_sem.at[0]),
        pltpu.make_async_copy(row, s_up, row_sem.at[1]),
    ]
    for c in finish:
        c.start()
    for c in started + finish:
        c.wait()


def shards(train_gate, train_up, train_down, router_weight, router_gain):
    n, groups = lax.axis_size("fsdp"), lax.axis_size("ep")
    experts, d, f = train_gate.shape
    rows = f // n
    tiles = rows // 8
    bf16, f32 = jnp.bfloat16, jnp.float32
    any_, vmem = pl.BlockSpec(memory_space=pl.ANY), pl.BlockSpec(memory_space=pltpu.VMEM)
    dma = pltpu.SemaphoreType.DMA
    columns = router_weight.shape[1]
    ready, last, scales, served = pl.pallas_call(
        functools.partial(exchange, n, groups, rows),
        out_shape=(
            pltpu.VMEM((3 * experts - 1, tiles, n, 8, d), bf16),
            pltpu.VMEM((n, tiles, 8, d), bf16),
            pltpu.VMEM((3, experts, rows), f32),
            pltpu.VMEM((groups, n, columns, d), bf16),
        ),
        in_specs=[any_] * 5,
        out_specs=(vmem,) * 4,
        scratch_shapes=[
            pltpu.VMEM((experts, f, d), f32),
            pltpu.VMEM((2 * experts, d, f), f32),
            pltpu.VMEM((columns, d), f32),
            pltpu.VMEM((1, d), f32),
            pltpu.VMEM((3 * experts, n, tiles, 8, d), bf16),
            pltpu.VMEM((3 * experts - 1, n, tiles, 8, d), bf16),
            pltpu.VMEM((columns, d), bf16),
            dma((3 * experts,)), dma((n,)), dma((2,)), dma((3 * experts,)), dma((3 * experts,)),
            dma, dma, dma, dma, dma, dma,
        ],
        compiler_params=pltpu.CompilerParams(
            collective_id=0, has_side_effects=True, vmem_limit_bytes=48 * MIB
        ),
        name="exchange",
    )(train_down, train_gate, train_up, router_weight.T, router_gain.reshape(1, d))
    tile = jax.ShapeDtypeStruct((experts, tiles, n, 8, d), bf16)
    scale = jax.ShapeDtypeStruct((experts, rows), f32)
    down, gate, up, s_down, s_gate, s_up, router = pl.pallas_call(
        write_out,
        out_shape=(tile, tile, tile, scale, scale, scale, jax.ShapeDtypeStruct(served.shape, bf16)),
        in_specs=[vmem] * 4,
        out_specs=(any_,) * 7,
        scratch_shapes=[
            pltpu.VMEM((tiles, n, 8, d), bf16),
            pltpu.VMEM((experts, rows), f32),
            dma((3 + 3 * ((experts + 1) // 2),)),
            dma((2,)),
        ],
        compiler_params=pltpu.CompilerParams(vmem_limit_bytes=16 * MIB),
        name="write_out",
    )(ready, last, scales, served)

    def whole(x):
        return x.transpose(0, 1, 3, 2, 4).reshape(experts, rows, n * d)

    serve_router = router.transpose(1, 3, 0, 2).reshape(n * d, -1)
    return (
        whole(gate).swapaxes(1, 2), whole(up).swapaxes(1, 2), whole(down),
        s_gate, s_up, s_down, serve_router,
    )


def solution(mesh):
    in_specs = (
        P("ep", "fsdp", None),
        P("ep", "fsdp", None),
        P("ep", None, "fsdp"),
        P("fsdp", "ep"),
        P("fsdp"),
    )
    out_specs = (
        P("ep", None, "fsdp"),
        P("ep", None, "fsdp"),
        P("ep", "fsdp", None),
        P("ep", "fsdp"),
        P("ep", "fsdp"),
        P("ep", "fsdp"),
        P(),
    )
    return jax.shard_map(shards, mesh=mesh, in_specs=in_specs, out_specs=out_specs, check_vma=False)
```

time: 109 us -> 107 us (0.982)
  Pallas kernels: 108 us -> 105 us
    pallas_call x1, Pallas kernels: 104 us -> 102 us  [shards(): pl.pallas_call(functools.partial(exchange, n, groups, rows), out_shape=(p...]
where the time goes in v2:
time: 107 us; the launch traced here: 106 us
  Pallas kernels  105 us (98%)
    pallas_call x1, Pallas kernels, shards(): pl.pallas_call(functools.partial(exchange, n, groups, rows), out_shape=(p...  102 us
    pallas_call x1, Pallas kernels, shards(): pl.pallas_call(write_out, out_shape=(tile, tile, tile, scale, scale, scal...  3.6 us

profile of v2, /device:TPU:0, one launch (start us, length us, event | category | flops | bytes accessed | tf_op | source)
XLA Modules:
  0.0 105.8 jit_solution(16668020050238230763)
XLA Ops:
  0.6 101.5 %exchange.1 = (bf16[23,11,16,8,128]{4,3,2,1,0:T(8,128)(2,1)S(1)}, bf16[16,11,8,128]{3,2,1,0:T(8,128)(2,1)S(1)}, f32[3,8,88]{2,1,0:T(8,128)S(1)}, bf16[8,16,8,128]{3,2,1,0:T(8,128)(2,1)S(1)}) custom-call(f32[8,1408,128]{2,1,0:T(8,128)} %down.1, f32[8,128,1408]{2,1,0:T(8,128)} %gate.1, f32[8,128,1408]{2,1,0:T(8,128)} %up.1, f32[8,128]{1,0:T(8,128)} %bitcast.18, ...), custom_call_target="tpu_custom_call" | custom-call | tf_op jit(solution)/shard_map/exchange/pallas_call | solution.py:280
  102.2 3.6 %write_out.1 = (bf16[8,11,16,8,128]{4,3,2,1,0:T(8,128)(2,1)}, bf16[8,11,16,8,128]{4,3,2,1,0:T(8,128)(2,1)}, bf16[8,11,16,8,128]{4,3,2,1,0:T(8,128)(2,1)}, f32[8,...) custom-call(bf16[23,11,16,8,128]{4,3,2,1,0:T(8,128)(2,1)S(1)} %get-tuple-element.18.ready, ...), custom_call_target="tpu_custom_call" | custom-call | tf_op jit(solution)/shard_map/write_out/pallas_call | solution.py:308

commit v3 on v2

v3 whole, which is shorter than its diff:
```python
import functools
import math

import jax
import jax.numpy as jnp
from jax import lax
from jax.experimental import pallas as pl
from jax.experimental.pallas import tpu as pltpu
from jax.sharding import PartitionSpec as P

MESH = pl.DeviceIdType.MESH
MIB = 2**20
FIRST = 4
GROUP = 4


def rings(side):
    by_distance = [[] for _ in range(2 * (side // 2) + 1)]
    for dy in range(side):
        for dx in range(side):
            by_distance[min(dy, side - dy) + min(dx, side - dx)].append((dy, dx))
    return by_distance[1:]


def scaled(arrived, put):
    n, tiles, eight, slab = arrived.shape
    total = jnp.abs(arrived[0].astype(jnp.float32))
    for s in range(1, n):
        total += jnp.abs(arrived[s].astype(jnp.float32))
    mean = jnp.sum(total, axis=2, keepdims=True) * (1.0 / (slab * n))
    inverse = 1.0 / mean
    for s in range(n):
        put(s, (arrived[s].astype(jnp.float32) * inverse).astype(jnp.bfloat16))
    row = jnp.sum(total.reshape(tiles * eight, slab).T, axis=0, keepdims=True)
    return row * (1.0 / (slab * n))


def exchange(
    n, groups, rows,
    down, gate, up, router, gain,
    ready, last, scales, served,
    down_in, wide_in, router_in, gain_in, send, recv, part,
    load_sem, head_sem, here_sem, send_sem, recv_sem, row_sem, in_sem, out_sem,
):
    me, group = lax.axis_index("fsdp"), lax.axis_index("ep")
    experts, tiles, slab = down_in.shape[0], rows // 8, down_in.shape[2]
    pieces = 3 * experts
    bf16 = jnp.bfloat16
    side = math.isqrt(n)
    away = rings(side)
    everyone = [place for ring in away for place in ring]

    def peer_of(place):
        dy, dx = place
        return lax.rem(me // side + dy, side) * side + lax.rem(me + dx, side)

    def wait_for(ref, sem):
        pltpu.make_async_copy(ref, ref, sem).wait()

    def tell_neighbours(sem):
        for place in away[0]:
            pl.semaphore_signal(sem, inc=1, device_id={"fsdp": peer_of(place)}, device_id_type=MESH)

    barrier = pltpu.get_barrier_semaphore()
    tell_neighbours(barrier)

    @pl.when(group == 0)
    def _():
        for g in range(1, groups):
            pl.semaphore_signal(barrier, inc=1, device_id={"ep": g}, device_id_type=MESH)

    def load_slab(place, sem):
        at = pl.ds(pl.multiple_of(peer_of(place) * rows, 8), rows)
        return pltpu.make_async_copy(down.at[0, at], down_in.at[0, at], head_sem.at[sem])

    def load(kind, e):
        src = (down, gate, up)[kind].at[e]
        dst = down_in.at[e] if kind == 0 else wide_in.at[(kind - 1) * experts + e]
        return pltpu.make_async_copy(src, dst, load_sem.at[lax.rem(kind * experts + e, FIRST)])

    near = len(away[0])
    for place in away[0]:
        load_slab(place, 0).start()
    for place in everyone[near:] + [(0, 0)]:
        load_slab(place, 1).start()
    for e in range(1, FIRST + 1):
        load(0, e).start()
    load_router = pltpu.make_async_copy(router, router_in, head_sem.at[2])
    load_gain = pltpu.make_async_copy(gain, gain_in, head_sem.at[3])
    load_router.start()
    load_gain.start()

    def row_copy(place):
        return pltpu.make_async_remote_copy(
            src_ref=part, dst_ref=served.at[group, me],
            send_sem=row_sem.at[0], recv_sem=row_sem.at[1],
            device_id={"fsdp": peer_of(place)}, device_id_type=MESH,
        )

    def share_copy(p, sem, place, final=False):
        peer = peer_of(place)
        return pltpu.make_async_remote_copy(
            src_ref=send.at[p, peer],
            dst_ref=last.at[me] if final else recv.at[p, me],
            send_sem=send_sem.at[0], recv_sem=recv_sem.at[sem],
            device_id={"fsdp": peer}, device_id_type=MESH,
        )

    def narrow_slab(e, k):
        x = down_in[e, pl.ds(pl.multiple_of(k * rows, 8), rows), :]
        send[e, k] = x.reshape(tiles, 8, slab).astype(bf16)

    def narrow_ring(e, ring):
        for place in ring:
            narrow_slab(e, peer_of(place))

    def send_ring(e, ring):
        for place in ring:
            share_copy(e, 0, place).start()

    wait_for(down_in.at[0, pl.ds(0, near * rows)], head_sem.at[0])
    narrow_ring(0, away[0])
    pl.semaphore_wait(barrier, near + jnp.where(group == 0, 0, 1))
    for hop in range(len(away)):
        if hop > 0:
            pl.semaphore_wait(here_sem.at[hop - 1], near)
        if hop < len(away) - 1:
            tell_neighbours(here_sem.at[hop])
        send_ring(0, away[hop])
        for e in range(1, FIRST):
            if hop == 0:
                load(0, e).wait()
                if e < FIRST - 1:
                    load(0, e + FIRST).start()
            narrow_ring(e, away[hop])
            send_ring(e, away[hop])
        if hop == 0:
            wait_for(down_in.at[0, pl.ds(0, (n - near) * rows)], head_sem.at[1])
        if hop < len(away) - 1:
            narrow_ring(0, away[hop + 1])
    for e in range(FIRST):
        narrow_slab(e, me)
        recv[e, me] = send[e, me]

    def send_all(p, sem):
        for place in everyone[::-1]:
            share_copy(p, sem, place).start()
        recv[p, me] = send[p, me]

    def load_ahead(kind, e):
        @pl.when(e + FIRST - 1 < experts)
        def _():
            load(kind, e + FIRST - 1).start()

        if kind < 2:

            @pl.when(e + FIRST - 1 >= experts)
            def _():
                load(kind + 1, e + FIRST - 1 - experts).start()

    def narrow_down(e, carry):
        load_ahead(0, e)
        load(0, e).wait()
        for k in range(n):
            narrow_slab(e, k)
        send_all(e, e // GROUP)
        return carry

    lax.fori_loop(FIRST, experts, narrow_down, 0)

    load_router.wait()
    load_gain.wait()
    part[...] = (router_in[...] * gain_in[...]).astype(bf16)
    served[group, me] = part[...]
    for place in everyone:
        row_copy(place).start()

    def narrow_wide(kind, e):
        load_ahead(kind, e)
        load(kind, e).wait()
        p = kind * experts + e
        for b in range(rows * n // slab):
            x = wide_in[p - experts, :, slab * b : slab * (b + 1)].T
            for i in range(slab // 8):
                at = (slab * b) // 8 + i
                send[p, at // tiles, at % tiles] = x[8 * i : 8 * (i + 1), :].astype(bf16)

    def narrow_gate(e, carry):
        narrow_wide(1, e)
        send_all(experts + e, (experts + e) // GROUP)
        return carry

    lax.fori_loop(0, experts, narrow_gate, 0)

    others = served.at[group, pl.ds(0, n - 1)]
    wait_for(others, row_sem.at[1])
    inward = pltpu.make_async_remote_copy(
        src_ref=served.at[group], dst_ref=served.at[group],
        send_sem=in_sem.at[0], recv_sem=in_sem.at[1],
        device_id={"ep": 0}, device_id_type=MESH,
    )

    def outward(g, j):
        return pltpu.make_async_remote_copy(
            src_ref=served.at[j], dst_ref=served.at[j],
            send_sem=out_sem.at[0], recv_sem=out_sem.at[1],
            device_id={"ep": g}, device_id_type=MESH,
        )

    @pl.when(group != 0)
    def _():
        inward.start()

    whole = pieces // GROUP - 1

    def narrow_up(e, carry):
        narrow_wide(2, e)

        @pl.when(e < experts - 1)
        def _():
            send_all(2 * experts + e, 2 * experts // GROUP + e // GROUP + (e + 2) // experts)

        return carry

    lax.fori_loop(0, experts, narrow_up, 0)
    for place in everyone[::-1]:
        share_copy(pieces - 1, whole + 2, place, final=True).start()
    last[me] = send[pieces - 1, me]

    theirs = served.at[pl.ds(0, groups - 1)]

    @pl.when(group == 0)
    def _():
        wait_for(theirs, in_sem.at[1])
        for g in range(1, groups):
            for j in range(groups):
                if j != g:
                    outward(g, j).start()

    def scale(p, carry):
        def put(s, x):
            ready[p, :, s] = x

        scales[p // experts, pl.ds(lax.rem(p, experts), 1), :] = scaled(recv.at[p], put)
        return carry

    for sem, (p, count) in enumerate(
        [(GROUP * g, GROUP) for g in range(whole)] + [(GROUP * whole, GROUP - 2), (pieces - 2, 1)]
    ):
        wait_for(recv.at[pl.ds(p, count), pl.ds(0, n - 1)], recv_sem.at[sem])
        lax.fori_loop(p, p + count, scale, 0)

    wait_for(others, row_sem.at[0])

    @pl.when(group == 0)
    def _():
        for _ in range(1, groups):
            wait_for(theirs, out_sem.at[0])

    @pl.when(group != 0)
    def _():
        wait_for(served.at[group], in_sem.at[0])
        wait_for(theirs, out_sem.at[1])

    wait_for(last.at[pl.ds(0, n - 1)], recv_sem.at[whole + 2])
    wait_for(send.at[pl.ds(0, pieces), pl.ds(0, n - 1)], send_sem.at[0])


def write_out(ready, last, scales, served, out_down, out_gate, out_up, s_down, s_gate, s_up, out_router, held, row, sem):
    experts = out_down.shape[0]
    copies = []
    for kind, out in enumerate((out_down, out_gate, out_up)):
        for e in range(experts - (kind == 2)):
            copies.append((ready.at[kind * experts + e], out.at[e], 0))
    copies += [(served, out_router, 1), (scales.at[0], s_down, 2), (scales.at[1], s_gate, 2)]
    for a, b, i in copies:
        pltpu.make_async_copy(a, b, sem.at[i]).start()

    def put(s, x):
        held[:, s] = x

    row[...] = scales[2]
    row[pl.ds(experts - 1, 1), :] = scaled(last, put)
    pltpu.make_async_copy(held, out_up.at[experts - 1], sem.at[3]).start()
    pltpu.make_async_copy(row, s_up, sem.at[4]).start()
    for i, ref in enumerate((ready, served, scales.at[pl.ds(0, 2)], held, row)):
        pltpu.make_async_copy(ref, ref, sem.at[i]).wait()


def shards(train_gate, train_up, train_down, router_weight, router_gain):
    n, groups = lax.axis_size("fsdp"), lax.axis_size("ep")
    experts, d, f = train_gate.shape
    rows = f // n
    tiles = rows // 8
    bf16, f32 = jnp.bfloat16, jnp.float32
    any_, vmem = pl.BlockSpec(memory_space=pl.ANY), pl.BlockSpec(memory_space=pltpu.VMEM)
    dma = pltpu.SemaphoreType.DMA
    columns = router_weight.shape[1]
    ready, last, scales, served = pl.pallas_call(
        functools.partial(exchange, n, groups, rows),
        out_shape=(
            pltpu.VMEM((3 * experts - 1, tiles, n, 8, d), bf16),
            pltpu.VMEM((n, tiles, 8, d), bf16),
            pltpu.VMEM((3, experts, rows), f32),
            pltpu.VMEM((groups, n, columns, d), bf16),
        ),
        in_specs=[any_] * 5,
        out_specs=(vmem,) * 4,
        scratch_shapes=[
            pltpu.VMEM((experts, f, d), f32),
            pltpu.VMEM((2 * experts, d, f), f32),
            pltpu.VMEM((columns, d), f32),
            pltpu.VMEM((1, d), f32),
            pltpu.VMEM((3 * experts, n, tiles, 8, d), bf16),
            pltpu.VMEM((3 * experts - 1, n, tiles, 8, d), bf16),
            pltpu.VMEM((columns, d), bf16),
            dma((FIRST,)), dma((4,)),
            pltpu.SemaphoreType.REGULAR((2 * (math.isqrt(n) // 2) - 1,)),
            dma((1,)), dma((3 * experts // GROUP + 2,)), dma((2,)), dma((2,)), dma((2,)),
        ],
        compiler_params=pltpu.CompilerParams(
            collective_id=0, has_side_effects=True, vmem_limit_bytes=48 * MIB
        ),
        name="exchange",
    )(train_down, train_gate, train_up, router_weight.T, router_gain.reshape(1, d))
    tile = jax.ShapeDtypeStruct((experts, tiles, n, 8, d), bf16)
    scale = jax.ShapeDtypeStruct((experts, rows), f32)
    down, gate, up, s_down, s_gate, s_up, router = pl.pallas_call(
        write_out,
        out_shape=(tile, tile, tile, scale, scale, scale, jax.ShapeDtypeStruct(served.shape, bf16)),
        in_specs=[vmem] * 4,
        out_specs=(any_,) * 7,
        scratch_shapes=[
            pltpu.VMEM((tiles, n, 8, d), bf16),
            pltpu.VMEM((experts, rows), f32),
            dma((5,)),
        ],
        compiler_params=pltpu.CompilerParams(vmem_limit_bytes=16 * MIB),
        name="write_out",
    )(ready, last, scales, served)

    def whole(x):
        return x.transpose(0, 1, 3, 2, 4).reshape(experts, rows, n * d)

    serve_router = router.transpose(1, 3, 0, 2).reshape(n * d, -1)
    return (
        whole(gate).swapaxes(1, 2), whole(up).swapaxes(1, 2), whole(down),
        s_gate, s_up, s_down, serve_router,
    )


def solution(mesh):
    in_specs = (
        P("ep", "fsdp", None),
        P("ep", "fsdp", None),
        P("ep", None, "fsdp"),
        P("fsdp", "ep"),
        P("fsdp"),
    )
    out_specs = (
        P("ep", None, "fsdp"),
        P("ep", None, "fsdp"),
        P("ep", "fsdp", None),
        P("ep", "fsdp"),
        P("ep", "fsdp"),
        P("ep", "fsdp"),
        P(),
    )
    return jax.shard_map(shards, mesh=mesh, in_specs=in_specs, out_specs=out_specs, check_vma=False)
```

time: 107 us -> 105 us (0.981)
    pallas_call x1, Pallas kernels: 102 us -> 100 us  [shards(): pl.pallas_call(functools.partial(exchange, n, groups, rows), out_shape=(p...]
where the time goes in v3:
time: 105 us; the launch traced here: 104 us
  Pallas kernels  104 us (99%)
    pallas_call x1, Pallas kernels, shards(): pl.pallas_call(functools.partial(exchange, n, groups, rows), out_shape=(p...  100 us
    pallas_call x1, Pallas kernels, shards(): pl.pallas_call(write_out, out_shape=(tile, tile, tile, scale, scale, scal...  3.48 us

profile of v3, /device:TPU:0, one launch (start us, length us, event | category | flops | bytes accessed | tf_op | source)
XLA Modules:
  0.0 104.3 jit_solution(18190622715365714680)
XLA Ops:
  0.6 100.2 %exchange.1 = (bf16[23,11,16,8,128]{4,3,2,1,0:T(8,128)(2,1)S(1)}, bf16[16,11,8,128]{3,2,1,0:T(8,128)(2,1)S(1)}, f32[3,8,88]{2,1,0:T(8,128)S(1)}, bf16[8,16,8,128]{3,2,1,0:T(8,128)(2,1)S(1)}) custom-call(f32[8,1408,128]{2,1,0:T(8,128)} %down.1, f32[8,128,1408]{2,1,0:T(8,128)} %gate.1, f32[8,128,1408]{2,1,0:T(8,128)} %up.1, f32[8,128]{1,0:T(8,128)} %bitcast.18, ...), custom_call_target="tpu_custom_call" | custom-call | tf_op jit(solution)/shard_map/exchange/pallas_call | solution.py:299
  100.8 3.5 %write_out.1 = (bf16[8,11,16,8,128]{4,3,2,1,0:T(8,128)(2,1)}, bf16[8,11,16,8,128]{4,3,2,1,0:T(8,128)(2,1)}, bf16[8,11,16,8,128]{4,3,2,1,0:T(8,128)(2,1)}, f32[8,...) custom-call(bf16[23,11,16,8,128]{4,3,2,1,0:T(8,128)(2,1)S(1)} %get-tuple-element.18.ready, ...), custom_call_target="tpu_custom_call" | custom-call | tf_op jit(solution)/shard_map/write_out/pallas_call | solution.py:328

commit v4 on v3

--- a/solution.py
+++ b/solution.py
@@ -84,7 +84,7 @@
     for place in everyone[near:] + [(0, 0)]:
         load_slab(place, 1).start()
     for e in range(1, FIRST + 1):
-        load(0, e).start()
+        load(e // experts, e % experts).start()
     load_router = pltpu.make_async_copy(router, router_in, head_sem.at[2])
     load_gain = pltpu.make_async_copy(gain, gain_in, head_sem.at[3])
     load_router.start()
@@ -116,7 +116,7 @@
 
     def send_ring(e, ring):
         for place in ring:
-            share_copy(e, 0, place).start()
+            share_copy(e, e // GROUP, place).start()
 
     wait_for(down_in.at[0, pl.ds(0, near * rows)], head_sem.at[0])
     narrow_ring(0, away[0])
@@ -131,11 +131,17 @@
             if hop == 0:
                 load(0, e).wait()
                 if e < FIRST - 1:
-                    load(0, e + FIRST).start()
+                    load((e + FIRST) // experts, (e + FIRST) % experts).start()
             narrow_ring(e, away[hop])
             send_ring(e, away[hop])
         if hop == 0:
             wait_for(down_in.at[0, pl.ds(0, (n - near) * rows)], head_sem.at[1])
+            load_router.wait()
+            load_gain.wait()
+            part[...] = (router_in[...] * gain_in[...]).astype(bf16)
+            served[group, me] = part[...]
+        for place in away[hop]:
+            row_copy(place).start()
         if hop < len(away) - 1:
             narrow_ring(0, away[hop + 1])
     for e in range(FIRST):
@@ -167,13 +173,6 @@
         return carry
 
     lax.fori_loop(FIRST, experts, narrow_down, 0)
-
-    load_router.wait()
-    load_gain.wait()
-    part[...] = (router_in[...] * gain_in[...]).astype(bf16)
-    served[group, me] = part[...]
-    for place in everyone:
-        row_copy(place).start()
 
     def narrow_wide(kind, e):
         load_ahead(kind, e)

time: 105 us -> 105 us (level)
  no operation moved by 1% of the time
where the time goes in v4:
time: 105 us; the launch traced here: 104 us
  Pallas kernels  104 us (99%)
    pallas_call x1, Pallas kernels, shards(): pl.pallas_call(functools.partial(exchange, n, groups, rows), out_shape=(p...  100 us
    pallas_call x1, Pallas kernels, shards(): pl.pallas_call(write_out, out_shape=(tile, tile, tile, scale, scale, scal...  3.48 us

profile of v4, /device:TPU:0, one launch (start us, length us, event | category | flops | bytes accessed | tf_op | source)
XLA Modules:
  0.0 104.3 jit_solution(6880384495337497633)
XLA Ops:
  0.6 100.2 %exchange.1 = (bf16[23,11,16,8,128]{4,3,2,1,0:T(8,128)(2,1)S(1)}, bf16[16,11,8,128]{3,2,1,0:T(8,128)(2,1)S(1)}, f32[3,8,88]{2,1,0:T(8,128)S(1)}, bf16[8,16,8,128]{3,2,1,0:T(8,128)(2,1)S(1)}) custom-call(f32[8,1408,128]{2,1,0:T(8,128)} %down.1, f32[8,128,1408]{2,1,0:T(8,128)} %gate.1, f32[8,128,1408]{2,1,0:T(8,128)} %up.1, f32[8,128]{1,0:T(8,128)} %bitcast.18, ...), custom_call_target="tpu_custom_call" | custom-call | tf_op jit(solution)/shard_map/exchange/pallas_call | solution.py:298
  100.8 3.5 %write_out.1 = (bf16[8,11,16,8,128]{4,3,2,1,0:T(8,128)(2,1)}, bf16[8,11,16,8,128]{4,3,2,1,0:T(8,128)(2,1)}, bf16[8,11,16,8,128]{4,3,2,1,0:T(8,128)(2,1)}, f32[8,...) custom-call(bf16[23,11,16,8,128]{4,3,2,1,0:T(8,128)(2,1)S(1)} %get-tuple-element.18.ready, ...), custom_call_target="tpu_custom_call" | custom-call | tf_op jit(solution)/shard_map/write_out/pallas_call | solution.py:327

commit v5 on v4

--- a/solution.py
+++ b/solution.py
@@ -169,7 +169,11 @@
         load(0, e).wait()
         for k in range(n):
             narrow_slab(e, k)
-        send_all(e, e // GROUP)
+
+        @pl.when(e > FIRST)
+        def _():
+            send_all(e - 1, (e - 1) // GROUP)
+
         return carry
 
     lax.fori_loop(FIRST, experts, narrow_down, 0)
@@ -186,7 +190,7 @@
 
     def narrow_gate(e, carry):
         narrow_wide(1, e)
-        send_all(experts + e, (experts + e) // GROUP)
+        send_all(experts + e - 1, (experts + e - 1) // GROUP)
         return carry
 
     lax.fori_loop(0, experts, narrow_gate, 0)
@@ -214,11 +218,8 @@
 
     def narrow_up(e, carry):
         narrow_wide(2, e)
-
-        @pl.when(e < experts - 1)
-        def _():
-            send_all(2 * experts + e, 2 * experts // GROUP + e // GROUP + (e + 2) // experts)
-
+        before = 2 * experts + e - 1
+        send_all(before, before // GROUP + (e + 1) // experts)
         return carry
 
     lax.fori_loop(0, experts, narrow_up, 0)

time: 105 us -> 105 us (level)
  no operation moved by 1% of the time
where the time goes in v5:
time: 105 us; the launch traced here: 104 us
  Pallas kernels  104 us (99%)
    pallas_call x1, Pallas kernels, shards(): pl.pallas_call(functools.partial(exchange, n, groups, rows), out_shape=(p...  100 us
    pallas_call x1, Pallas kernels, shards(): pl.pallas_call(write_out, out_shape=(tile, tile, tile, scale, scale, scal...  3.48 us

profile of v5, /device:TPU:0, one launch (start us, length us, event | category | flops | bytes accessed | tf_op | source)
XLA Modules:
  0.0 104.3 jit_solution(4546333101237642997)
XLA Ops:
  0.6 100.2 %exchange.1 = (bf16[23,11,16,8,128]{4,3,2,1,0:T(8,128)(2,1)S(1)}, bf16[16,11,8,128]{3,2,1,0:T(8,128)(2,1)S(1)}, f32[3,8,88]{2,1,0:T(8,128)S(1)}, bf16[8,16,8,128]{3,2,1,0:T(8,128)(2,1)S(1)}) custom-call(f32[8,1408,128]{2,1,0:T(8,128)} %down.1, f32[8,128,1408]{2,1,0:T(8,128)} %gate.1, f32[8,128,1408]{2,1,0:T(8,128)} %up.1, f32[8,128]{1,0:T(8,128)} %bitcast.18, ...), custom_call_target="tpu_custom_call" | custom-call | tf_op jit(solution)/shard_map/exchange/pallas_call | solution.py:299
  100.8 3.5 %write_out.1 = (bf16[8,11,16,8,128]{4,3,2,1,0:T(8,128)(2,1)}, bf16[8,11,16,8,128]{4,3,2,1,0:T(8,128)(2,1)}, bf16[8,11,16,8,128]{4,3,2,1,0:T(8,128)(2,1)}, f32[8,...) custom-call(bf16[23,11,16,8,128]{4,3,2,1,0:T(8,128)(2,1)S(1)} %get-tuple-element.18.ready, ...), custom_call_target="tpu_custom_call" | custom-call | tf_op jit(solution)/shard_map/write_out/pallas_call | solution.py:328

commit v6 on v5

--- a/solution.py
+++ b/solution.py
@@ -11,7 +11,7 @@
 MESH = pl.DeviceIdType.MESH
 MIB = 2**20
 FIRST = 4
-GROUP = 4
+GROUP = 8
 
 
 def rings(side):
@@ -47,12 +47,14 @@
     pieces = 3 * experts
     bf16 = jnp.bfloat16
     side = math.isqrt(n)
+    row, column = me // side, lax.rem(me, side)
+    sign = 1 - 2 * lax.rem(row + column + group, 2)
     away = rings(side)
     everyone = [place for ring in away for place in ring]
 
     def peer_of(place):
         dy, dx = place
-        return lax.rem(me // side + dy, side) * side + lax.rem(me + dx, side)
+        return lax.rem(row + sign * dy + side, side) * side + lax.rem(column + sign * dx + side, side)
 
     def wait_for(ref, sem):
         pltpu.make_async_copy(ref, ref, sem).wait()

time: 105 us -> 105 us (level)
  no operation moved by 1% of the time
where the time goes in v6:
time: 105 us; the launch traced here: 104 us
  Pallas kernels  104 us (99%)
    pallas_call x1, Pallas kernels, shards(): pl.pallas_call(functools.partial(exchange, n, groups, rows), out_shape=(p...  100 us
    pallas_call x1, Pallas kernels, shards(): pl.pallas_call(write_out, out_shape=(tile, tile, tile, scale, scale, scal...  3.48 us

profile of v6, /device:TPU:0, one launch (start us, length us, event | category | flops | bytes accessed | tf_op | source)
XLA Modules:
  0.0 104.3 jit_solution(4789143397873467982)
XLA Ops:
  0.6 100.1 %exchange.1 = (bf16[23,11,16,8,128]{4,3,2,1,0:T(8,128)(2,1)S(1)}, bf16[16,11,8,128]{3,2,1,0:T(8,128)(2,1)S(1)}, f32[3,8,88]{2,1,0:T(8,128)S(1)}, bf16[8,16,8,128]{3,2,1,0:T(8,128)(2,1)S(1)}) custom-call(f32[8,1408,128]{2,1,0:T(8,128)} %down.1, f32[8,128,1408]{2,1,0:T(8,128)} %gate.1, f32[8,128,1408]{2,1,0:T(8,128)} %up.1, f32[8,128]{1,0:T(8,128)} %bitcast.18, ...), custom_call_target="tpu_custom_call" | custom-call | tf_op jit(solution)/shard_map/exchange/pallas_call | solution.py:301
  100.8 3.5 %write_out.1 = (bf16[8,11,16,8,128]{4,3,2,1,0:T(8,128)(2,1)}, bf16[8,11,16,8,128]{4,3,2,1,0:T(8,128)(2,1)}, bf16[8,11,16,8,128]{4,3,2,1,0:T(8,128)(2,1)}, f32[8,...) custom-call(bf16[23,11,16,8,128]{4,3,2,1,0:T(8,128)(2,1)S(1)} %get-tuple-element.18.ready, ...), custom_call_target="tpu_custom_call" | custom-call | tf_op jit(solution)/shard_map/write_out/pallas_call | solution.py:330
